TPU v7x, 32 devices: a whole 2x2x4 slice. The times are simulated.
32 devices in a mesh: prow: 4 (over y, core), pcol: 8 (over z, x).
Axes of the slice: x: 2, y: 2, z: 4, core: 2. Of those that a mesh axis runs over, the one named last changes fastest.
Arguments:
- tiles: bfloat16 [4, 8, 16, 256, 256], P('prow', 'pcol'), may hold values from -6 to 6
- tile_ids: int32 [4, 8, 16], P('prow', 'pcol'), may hold values from 0 to 127, as said below
- counts: int32 [4, 8], P('prow', 'pcol'), may hold values from 1 to 16, as said below
- pivots: int32 [256], replicated, may hold values from 0 to 16383, as said below
- l_inverse: bfloat16 [256, 256], P(None, 'pcol'), may hold values from -1 to 1, as said below
- u_inverse: bfloat16 [256, 256], P('prow'), may hold values from -0.125 to 0.5, as said below
Outputs:
- factored: bfloat16 [4, 8, 16, 256, 256], P('prow', 'pcol')
Inputs may be any that keep to these rules, and one draw needn't show every extreme that they name: Live slot s of device (p, q) holds local tile row tile_ids[p, q, s] // 8 and local tile column tile_ids[p, q, s] % 8; live codes of one device are distinct, padded slots hold arbitrary codes. Let R be the tile rows I >= 1 with tile (I, 0) held and C the tile columns J >= 1 with tile (0, J) held. Tile (0, 0) is held; on each prow index R takes the last one to 3 local tile rows, on each pcol index C takes the last one to 3 local tile columns, and both most counts are reached on some index. Every tile whose row is 0 or in R and whose column is 0 or in C is held; no other held tile lies in tile row 0, a tile row of R, or tile column 0. `counts`: some device has 16 live slots. Row r of tile row 0 and row pivots[r] change places; pivots[r] is r or a row of a tile row of R, and the values that differ from their r are distinct. `l_inverse`: lower triangular with unit diagonal. `u_inverse`: upper triangular with a positive diagonal.
All inputs are finite; a program needn't handle non-finite values.
Results may differ from a plain program's by a relative error of at most 0.0056.
Values may be sent and summed in bfloat16 or wider, within the bound.
A program may use at most 64 MiB of HBM per device.

v0:
```python
import functools

import jax
import jax.numpy as jnp
from jax import lax
from jax.experimental import pallas as pl
from jax.experimental.pallas import tpu as pltpu
from jax.sharding import PartitionSpec as P

LOCAL_ROWS = 16
LOWER_MOST = 3
UPPER_MOST = 3
MESH = pl.DeviceIdType.MESH
NT = (((1,), (1,)), ((), ()))
TN = (((0,), (0,)), ((), ()))
FAR = 1 << 24


def dot(a, b, dims=None):
    if dims is None:
        return jnp.dot(a, b, preferred_element_type=jnp.float32)
    return lax.dot_general(a, b, dims, preferred_element_type=jnp.float32)


def kernel(
    rows, cols, grid_cols,
    ids_ref, counts_ref, piv_ref, l_ref, u_ref, tiles_ref,
    out_ref,
    store, part, old, send, recv, raw, top, lt, uf, new,
    tile_sem, ss, rs,
):
    side = piv_ref.shape[1]
    half = side // 2
    slots = tiles_ref.shape[2]
    zero_at = store.shape[0] - 1
    levels = rows.bit_length() - 1
    width = UPPER_MOST + 1
    height = LOWER_MOST + 1
    pieces = min(cols, 16)
    p = lax.axis_index("prow")
    q = lax.axis_index("pcol")
    core = lax.rem(p, 2)
    used = [0]
    ends = []

    def fresh(n=1):
        used[0] += n
        return used[0] - n

    def remote(src, dst, index, device):
        return pltpu.make_async_remote_copy(
            src_ref=src, dst_ref=dst, send_sem=ss.at[index], recv_sem=rs.at[index],
            device_id=device, device_id_type=MESH,
        )

    def guard(cond, fn):
        if cond is None:
            fn()
        else:
            pl.when(cond)(fn)

    def begin(cond, make):
        guard(cond, lambda: make().start())
        ends.append((cond, make))

    tile_copy = pltpu.make_async_copy(tiles_ref.at[0, 0], store.at[pl.ds(0, slots)], tile_sem)
    tile_copy.start()

    barrier = pltpu.get_barrier_semaphore()
    for d in range(1, rows):
        pl.semaphore_signal(barrier, inc=1, device_id={"prow": lax.rem(p + d, rows)}, device_id_type=MESH)
    for d in range(1, cols):
        pl.semaphore_signal(barrier, inc=1, device_id={"pcol": lax.rem(q + d, cols)}, device_id_type=MESH)

    first_row = LOCAL_ROWS - LOWER_MOST
    first_col = grid_cols - UPPER_MOST
    packed = [jnp.int32(0)] * height
    source = []
    live_count = counts_ref[0, 0]
    for s in range(slots):
        code = ids_ref[0, 0, s]
        row = code // grid_cols
        col = code - row * grid_cols
        live = s < live_count
        c = jnp.where((col == 0) & (q == 0), 0, jnp.where(col >= first_col, col - first_col + 1, -1))
        k = jnp.where((row == 0) & (p == 0), 0, jnp.where(row >= first_row, row - first_row + 1, -1))
        weight = jnp.int32(0)
        for j in range(width):
            weight = jnp.where(c == j, (s + 1) << (5 * j), weight)
        for i in range(height):
            packed[i] = packed[i] + jnp.where((k == i) & live, weight, 0)
        structural = (c >= 0) & (k >= 0)
        source.append(jnp.where(live, jnp.where(structural, slots + k * width + c, s), zero_at))

    def tile(k, c):
        slot = (packed[k] >> (5 * c)) & 31
        return store[jnp.where(slot > 0, slot - 1, zero_at)]

    store[zero_at] = jnp.zeros((side, side), jnp.bfloat16)
    piece = lt.shape[1]
    eye = (lax.broadcasted_iota(jnp.int32, (piece, piece), 0)
           == lax.broadcasted_iota(jnp.int32, (piece, piece), 1)).astype(jnp.float32).astype(jnp.bfloat16)
    lt[q] = dot(eye, l_ref[...], NT).astype(lt.dtype)
    u_rows = u_ref.shape[0]

    def u_part(at):
        return uf.at[pl.ds(pl.multiple_of(at * u_rows, 16), u_rows)]

    uf[pl.ds(pl.multiple_of(p * u_rows, 16), u_rows)] = u_ref[...]

    piv_lanes = jnp.broadcast_to(piv_ref[...], (side, side))
    piv_rows = piv_lanes.T
    lane = lax.broadcasted_iota(jnp.int32, (side, side), 1)
    sub = lax.broadcasted_iota(jnp.int32, (side, side), 0)
    base = [jnp.where(p == 0, 0, -FAR)]
    for i in range(LOWER_MOST):
        base.append((p + rows * (first_row + i)) * side)
    pick = [(piv_rows == lane + b).astype(jnp.float32).astype(jnp.bfloat16) for b in base]
    owner_high = lax.rem(piv_rows // side, rows) >= rows // 2

    pl.semaphore_wait(barrier, rows + cols - 2)

    l_sem = fresh(cols)
    u_sem = fresh(rows)
    for d in range(1, rows):
        begin(None, lambda d=d: remote(u_ref, u_part(p), u_sem + d, {"prow": lax.rem(p + d, rows)}))
    for d in range(1, cols):
        begin(None, lambda d=d: remote(lt.at[q], lt.at[q], l_sem + d, {"pcol": lax.rem(q + d, cols)}))
    tile_copy.wait()

    def row_cast(buf):
        length = buf.shape[0] // pieces
        scatter = fresh(pieces)
        gather = fresh(cols)

        def at(j):
            return buf.at[pl.ds(pl.multiple_of(j * length, 16), length)]

        def relay():
            for d in range(1, cols):
                to = lax.rem(q + d, cols)
                begin((to != 0) & (q < pieces),
                      lambda d=d, to=to: remote(at(q), at(q), gather + d, {"pcol": to}))

        def root():
            for j in range(1, pieces):
                begin(q == 0, lambda j=j: remote(at(j), at(j), scatter + j, {"pcol": j}))

        def arrive():
            for j in range(1, pieces):
                guard(q == j, lambda j=j: remote(at(j), at(j), scatter + j, {"pcol": 0}).wait_recv())

        def finish():
            for d in range(1, cols):
                frm = lax.rem(q + cols - d, cols)
                guard((q != 0) & (frm < pieces),
                      lambda d=d, frm=frm: remote(at(frm), at(frm), gather + d, {"pcol": frm}).wait_recv())

        return root, arrive, relay, finish

    raw_root, raw_arrive, raw_relay, raw_finish = row_cast(raw)
    top_root, top_arrive, top_relay, top_finish = row_cast(top)

    @pl.when(q == 0)
    def _():
        for i in range(LOWER_MOST):
            raw[pl.ds(i * side, side)] = tile(i + 1, 0)

    raw_root()

    def only(c):
        return (q == 0) if c == 0 else None

    def both(a, b):
        return b if a is None else (a if b is None else a & b)

    def part_rows(buf, at):
        return buf.at[pl.ds(pl.multiple_of(at * half, 16), half)]

    partner = {"prow": p + 1 - 2 * core}
    level0 = [fresh(2) for c in range(width)]
    for c in range(width):
        def contribute(c=c):
            total = dot(pick[0], tile(0, c))
            for k in range(1, height):
                total = total + dot(pick[k], tile(k, c))
            part[c] = total.astype(jnp.bfloat16)

            @pl.when(p == 0)
            def _():
                old[c] = tile(0, c)

        guard(only(c), contribute)
        begin(only(c), lambda c=c: remote(part.at[c], recv.at[0, c], level0[c], partner))
        begin(both(only(c), p == 0), lambda c=c: remote(old.at[c], old.at[c], level0[c] + 1, {"prow": 1}))

    def low(level):
        return p < (1 << level)

    def high(level):
        return (p >= (1 << level)) & (p < (2 << level))

    sems = {}

    def level_send(level, c):
        peer = {"prow": p + (1 << level) - 2 * (1 << level) * lax.rem(p // (1 << level), 2)}
        last = level == levels - 1
        sems[level, c] = fresh(4)
        index = sems[level, c]

        def build():
            if level == 1:
                @pl.when(p == 1)
                def _():
                    remote(old.at[c], old.at[c], level0[c] + 1, {"prow": 0}).wait_recv()
                remote(part.at[c], recv.at[0, c], level0[c], partner).wait_recv()
            total = part[c].astype(jnp.float32) + recv[level - 1, c].astype(jnp.float32)
            part_next = total.astype(jnp.bfloat16)
            send[level - 1, c] = part_next
            if last:
                @pl.when(p < rows // 2)
                def _():
                    new[c] = jnp.where(owner_high, old[c].astype(jnp.float32), total).astype(jnp.bfloat16)

                @pl.when(p >= rows // 2)
                def _():
                    new[c] = part_next

        guard(only(c), build)
        src = new.at[c] if last else send.at[level - 1, c]
        begin(only(c), lambda: remote(part_rows(src, core), part_rows(recv.at[level, c], core), index, peer))
        if not last:
            begin(both(only(c), low(level)),
                  lambda: remote(part_rows(old.at[c], core), part_rows(old.at[c], core), index + 1, peer))

    def level_forward(level, c):
        last = level == levels - 1
        index = sems[level, c]
        here = part_rows(recv.at[level, c], core)
        guard(only(c), lambda: remote(here, here, index, partner).wait_recv())
        begin(only(c), lambda: remote(here, here, index + 2, partner))
        if not last:
            mine = part_rows(old.at[c], core)
            guard(both(only(c), high(level)), lambda: remote(mine, mine, index + 1, partner).wait_recv())
            begin(both(only(c), high(level)), lambda: remote(mine, mine, index + 3, partner))

    def level_done(level, c):
        index = sems[level, c]
        there = part_rows(recv.at[level, c], 1 - core)
        guard(only(c), lambda: remote(there, there, index + 2, partner).wait_recv())
        if level < levels - 1:
            theirs = part_rows(old.at[c], 1 - core)
            guard(both(only(c), high(level)), lambda: remote(theirs, theirs, index + 3, partner).wait_recv())

    for level in range(1, levels):
        for c in range(width):
            if level > 1:
                def carry(c=c, level=level):
                    part[c] = send[level - 2, c]
                guard(only(c), carry)
            level_send(level, c)
        for c in range(width):
            level_forward(level, c)
        for c in range(width):
            level_done(level, c)
            if level == levels - 1 and c == 0:
                @pl.when((q == 0) & (p < rows // 2))
                def _():
                    top[...] = old[0]

                @pl.when((q == 0) & (p >= rows // 2))
                def _():
                    top[...] = recv[levels - 1, 0]

                top_root()
                guard(None, raw_arrive)
                raw_relay()
                top_arrive()
                top_relay()

    mine_high = p >= rows // 2
    for d in range(1, cols):
        frm = lax.rem(q + cols - d, cols)
        remote(lt.at[frm], lt.at[frm], l_sem + d, {"pcol": frm}).wait_recv()
    lower_t = lt[...].reshape(side, side).astype(jnp.bfloat16)

    same = (owner_high.astype(jnp.int32) == mine_high.astype(jnp.int32))

    def fresh_top(c):
        return jnp.where(same, send[levels - 2, c].astype(jnp.float32),
                         recv[levels - 1, c].astype(jnp.float32)).astype(jnp.bfloat16)

    @pl.when((q == 0) & (p == 0))
    def _():
        store[slots] = fresh_top(0)

    for c in range(1, width):
        store[slots + c] = dot(lower_t, fresh_top(c), TN).astype(jnp.bfloat16)

        @pl.when(mine_high)
        def _():
            old[c] = recv[levels - 1, c]

    def swap(k, block, source_rows):
        hit = piv_lanes == sub + base[k]
        moved = jnp.max(hit.astype(jnp.float32), axis=1, keepdims=True) > 0.5
        chosen = dot(hit.astype(jnp.float32).astype(jnp.bfloat16), source_rows)
        return jnp.where(moved, chosen, block.astype(jnp.float32))

    for d in range(1, rows):
        frm = lax.rem(p + rows - d, rows)
        remote(u_ref, u_part(frm), u_sem + d, {"prow": frm}).wait_recv()
    raw_finish()
    top_finish()
    for k in range(1, height):
        block = swap(k, raw[pl.ds((k - 1) * side, side)], top[...]).astype(jnp.bfloat16)
        lower = dot(block, uf[...]).astype(jnp.bfloat16)
        store[slots + k * width] = lower
        for c in range(1, width):
            value = swap(k, tile(k, c), old[c])
            store[slots + k * width + c] = (value - dot(lower, store[slots + c])).astype(jnp.bfloat16)

    for s in range(slots):
        out_ref[0, 0, s] = store[source[s]]
    for cond, make in ends:
        guard(cond, lambda make=make: make().wait_send())


def body(tiles, tile_ids, counts, pivots, l_inverse, u_inverse):
    rows = lax.axis_size("prow")
    cols = lax.axis_size("pcol")
    side = pivots.shape[0]
    slots = tiles.shape[2]
    grid_cols = LOCAL_ROWS * rows // cols
    levels = rows.bit_length() - 1
    width = UPPER_MOST + 1
    height = LOWER_MOST + 1
    piece = side // cols
    block = (side, side)
    pieces = min(cols, 16)
    count = rows + cols + 2 * (pieces + cols) + width * (2 + 4 * (levels - 1))
    kind = jnp.bfloat16
    vmem = pl.BlockSpec(memory_space=pltpu.VMEM)
    smem = pl.BlockSpec(memory_space=pltpu.SMEM)
    return pl.pallas_call(
        functools.partial(kernel, rows, cols, grid_cols),
        out_shape=jax.ShapeDtypeStruct(tiles.shape, tiles.dtype),
        in_specs=[smem, smem, vmem, vmem, vmem, pl.BlockSpec(memory_space=pl.ANY)],
        out_specs=vmem,
        scratch_shapes=[
            pltpu.VMEM((slots + height * width + 1,) + block, kind),
            pltpu.VMEM((width,) + block, kind),
            pltpu.VMEM((width,) + block, kind),
            pltpu.VMEM((levels - 1, width) + block, kind),
            pltpu.VMEM((levels, width) + block, kind),
            pltpu.VMEM((LOWER_MOST * side, side), kind),
            pltpu.VMEM(block, kind),
            pltpu.VMEM((cols, piece, side), kind if piece % 16 == 0 else jnp.float32),
            pltpu.VMEM(block, kind),
            pltpu.VMEM((width,) + block, kind),
            pltpu.SemaphoreType.DMA,
            pltpu.SemaphoreType.DMA((count,)),
            pltpu.SemaphoreType.DMA((count,)),
        ],
        compiler_params=pltpu.CompilerParams(
            collective_id=0, has_side_effects=True, vmem_limit_bytes=48 * 1024 * 1024
        ),
    )(tile_ids, counts, pivots.reshape(1, side), l_inverse, u_inverse, tiles)


def solution(mesh):
    placed = (
        P("prow", "pcol", None, None, None),
        P("prow", "pcol", None),
        P("prow", "pcol"),
        P(),
        P(None, "pcol"),
        P("prow", None),
    )
    return jax.shard_map(
        body,
        mesh=mesh,
        in_specs=placed,
        out_specs=P("prow", "pcol", None, None, None),
        check_vma=False,
    )
```

profile of v0, /device:TPU:26, one launch (start us, length us, event | category | flops | bytes accessed | tf_op | source)
XLA Modules:
  0.0 36.2 jit_solution(7034987538524299240)
XLA Ops:
  0.7 0.8 %copy.7.l_ref = bf16[256,32]{1,0:T(8,128)(2,1)S(1)} copy(bf16[256,32]{0,1:T(8,128)(2,1)} %param.10) | data formatting | bytes 32768 | tf_op args[4]
  1.5 0.0 copy-start
  1.5 1.6 %copy-done = bf16[1,1,16,256,256]{4,3,2,1,0:T(8,128)(2,1)S(1)} copy-done((bf16[1,1,16,256,256]{4,3,2,1,0:T(8,128)(2,1)S(1)}, bf16[1,1,16,256,256]{4,3,2,1,0:T(8,128)(2,1)}, u32[]{:S(2)}) %copy-start) | copy-done | bytes 2097176
  3.1 0.0 copy-start.1
  3.1 0.8 %copy-done.1 = bf16[64,256]{1,0:T(8,128)(2,1)S(1)} copy-done((bf16[64,256]{1,0:T(8,128)(2,1)S(1)}, bf16[64,256]{1,0:T(8,128)(2,1)}, u32[]{:S(2)}) %copy-start.1) | copy-done | bytes 32792
  3.8 0.0 copy-start.2
  3.8 0.7 %copy-done.2 = s32[256]{0:T(256)S(1)} copy-done((s32[256]{0:T(256)S(1)}, s32[256]{0:T(256)}, u32[]{:S(2)}) %copy-start.2) | copy-done | bytes 1048
  4.5 0.0 copy-start.3
  4.5 0.7 %copy-done.3 = s32[1,1,16]{2,1,0:T(1,128)S(1)} copy-done((s32[1,1,16]{2,1,0:T(1,128)S(1)}, s32[1,1,16]{2,1,0:T(1,128)}, u32[]{:S(2)}) %copy-start.3) | copy-done | bytes 88
  5.2 29.6 %shard_map.64 = bf16[1,1,16,256,256]{4,3,2,1,0:T(8,128)(2,1)S(1)} custom-call(s32[1,1,16]{2,1,0:T(1,128)S(1)} %copy-done.3, s32[1,1]{1,0:T(1,128)S(6)} %copy.9.counts_ref, s32[1,256]{1,0:T(1,128)S(1)} %bitcast.1, bf16[256,32]{1,0:T(8,128)(2,1)S(1)} %copy.7.l_ref, bf16[64,256]{1,0:T(8,128)(2,1)S(1)} %copy-done.1, bf16[1,1,16,256,256]{4,3,2,1,0:T(8,128)(2,1)S(1)} %copy-done), custom_call_target="tpu_custom_call" | custom-call | tf_op jit(solution)/shard_map/pallas_call | solution.py:345
  34.8 1.3 %copy.10 = bf16[1,1,16,256,256]{4,3,2,1,0:T(8,128)(2,1)} copy(bf16[1,1,16,256,256]{4,3,2,1,0:T(8,128)(2,1)S(1)} %shard_map.64) | data formatting | bytes 4194304
Async XLA Ops:
  1.5 1.6 %copy-start = (bf16[1,1,16,256,256]{4,3,2,1,0:T(8,128)(2,1)S(1)}, bf16[1,1,16,256,256]{4,3,2,1,0:T(8,128)(2,1)}, u32[]{:S(2)}) copy-start(bf16[1,1,16,256,256]{4,3,2,1,0:T(8,128)(2,1)} %tiles_ref.1) | copy-start | bytes 6291460
  3.1 0.8 %copy-start.1 = (bf16[64,256]{1,0:T(8,128)(2,1)S(1)}, bf16[64,256]{1,0:T(8,128)(2,1)}, u32[]{:S(2)}) copy-start(bf16[64,256]{1,0:T(8,128)(2,1)} %u_ref.1) | copy-start | bytes 98308
  3.8 0.7 %copy-start.2 = (s32[256]{0:T(256)S(1)}, s32[256]{0:T(256)}, u32[]{:S(2)}) copy-start(s32[256]{0:T(256)} %param.9) | copy-start | bytes 3076
  4.5 0.7 %copy-start.3 = (s32[1,1,16]{2,1,0:T(1,128)S(1)}, s32[1,1,16]{2,1,0:T(1,128)}, u32[]{:S(2)}) copy-start(s32[1,1,16]{2,1,0:T(1,128)} %ids_ref.1) | copy-start | bytes 196
where the time goes:
time: 36.7 us; the launch traced here: 36.2 us
  Pallas kernels  29.6 us (81%)
  local copies, waits for them, and re-layouts  5.84 us (16%)
  between operations  0.67 us (2%)
    pallas_call x1, Pallas kernels, body(): pl.pallas_call(functools.partial(kernel, rows, cols, grid_cols), out_shap...  29.6 us
    unnamed x10, local copies, waits for them, and re-layouts  5.84 us

commit v1 on v0

v1 whole, which is shorter than its diff:
```python
import functools

import jax
import jax.numpy as jnp
from jax import lax
from jax.experimental import pallas as pl
from jax.experimental.pallas import tpu as pltpu
from jax.sharding import PartitionSpec as P

LOCAL_ROWS = 16
LOWER_MOST = 3
UPPER_MOST = 3
MESH = pl.DeviceIdType.MESH
NT = (((1,), (1,)), ((), ()))
TN = (((0,), (0,)), ((), ()))
FAR = 1 << 24


def dot(a, b, dims=None):
    if dims is None:
        return jnp.dot(a, b, preferred_element_type=jnp.float32)
    return lax.dot_general(a, b, dims, preferred_element_type=jnp.float32)


def kernel(
    rows, cols, grid_cols,
    ids_hbm, counts_hbm, piv_hbm, l_hbm, u_hbm, tiles_hbm,
    out_ref,
    ids_ref, counts_ref, piv_ref,
    store, part, old, send, recv, new, raw, top, lt, uf, corner,
    in_sem, ss, rs,
):
    side = piv_ref.shape[1]
    half = side // 2
    slots = tiles_hbm.shape[2]
    zero_at = store.shape[0] - 1
    levels = rows.bit_length() - 1
    width = UPPER_MOST + 1
    height = LOWER_MOST + 1
    pieces = min(cols, 16)
    panel_cols = range(1, width)
    p = lax.axis_index("prow")
    q = lax.axis_index("pcol")
    core = lax.rem(p, 2)
    used = [0]
    ends = []

    def fresh(n=1):
        used[0] += n
        return used[0] - n

    def remote(src, dst, index, device):
        return pltpu.make_async_remote_copy(
            src_ref=src, dst_ref=dst, send_sem=ss.at[index], recv_sem=rs.at[index],
            device_id=device, device_id_type=MESH,
        )

    def guard(cond, fn):
        if cond is None:
            fn()
        else:
            pl.when(cond)(fn)

    def begin(cond, make):
        guard(cond, lambda: make().start())
        ends.append((cond, make))

    def arrived(cond, make):
        guard(cond, lambda: make().wait_recv())

    def span(buf, at, length):
        return buf.at[pl.ds(pl.multiple_of(at * length, 16), length)]

    u_rows = u_hbm.shape[0]
    tile_copy = pltpu.make_async_copy(tiles_hbm.at[0, 0], store.at[pl.ds(0, slots)], in_sem.at[0])
    inputs = [
        pltpu.make_async_copy(ids_hbm, ids_ref, in_sem.at[1]),
        pltpu.make_async_copy(counts_hbm, counts_ref, in_sem.at[2]),
        pltpu.make_async_copy(piv_hbm, piv_ref, in_sem.at[3]),
        pltpu.make_async_copy(l_hbm, lt.at[q], in_sem.at[4]),
        pltpu.make_async_copy(u_hbm, span(uf, p, u_rows), in_sem.at[5]),
    ]
    for copy in inputs[:3]:
        copy.start()
    tile_copy.start()
    for copy in inputs[3:]:
        copy.start()

    barrier = pltpu.get_barrier_semaphore()
    for d in range(1, rows):
        pl.semaphore_signal(barrier, inc=1, device_id={"prow": lax.rem(p + d, rows)}, device_id_type=MESH)
    for d in range(1, cols):
        pl.semaphore_signal(barrier, inc=1, device_id={"pcol": lax.rem(q + d, cols)}, device_id_type=MESH)
    store[zero_at] = jnp.zeros((side, side), jnp.bfloat16)
    for copy in inputs:
        copy.wait()

    first_row = LOCAL_ROWS - LOWER_MOST
    first_col = grid_cols - UPPER_MOST
    packed = [jnp.int32(0)] * height
    source = []
    live_count = counts_ref[0, 0]
    for s in range(slots):
        code = ids_ref[0, 0, s]
        row = code // grid_cols
        col = code - row * grid_cols
        live = s < live_count
        c = jnp.where((col == 0) & (q == 0), 0, jnp.where(col >= first_col, col - first_col + 1, -1))
        k = jnp.where((row == 0) & (p == 0), 0, jnp.where(row >= first_row, row - first_row + 1, -1))
        weight = jnp.int32(0)
        for j in range(width):
            weight = jnp.where(c == j, (s + 1) << (5 * j), weight)
        for i in range(height):
            packed[i] = packed[i] + jnp.where((k == i) & live, weight, 0)
        structural = (c >= 0) & (k >= 0)
        source.append(jnp.where(live, jnp.where(structural, slots + k * width + c, s), zero_at))

    def tile(k, c):
        slot = (packed[k] >> (5 * c)) & 31
        return store[jnp.where(slot > 0, slot - 1, zero_at)]

    piv_lanes = jnp.broadcast_to(piv_ref[...], (side, side))
    piv_rows = piv_lanes.T
    lane = lax.broadcasted_iota(jnp.int32, (side, side), 1)
    sub = lax.broadcasted_iota(jnp.int32, (side, side), 0)
    base = [jnp.where(p == 0, 0, -FAR)]
    for i in range(LOWER_MOST):
        base.append((p + rows * (first_row + i)) * side)
    pick = [(piv_rows == lane + b).astype(jnp.float32).astype(jnp.bfloat16) for b in base]
    owner_high = lax.rem(piv_rows // side, rows) >= rows // 2
    mine_high = p >= rows // 2
    same = owner_high.astype(jnp.int32) == mine_high.astype(jnp.int32)

    tile_copy.wait()

    @pl.when(q == 0)
    def _():
        for i in range(LOWER_MOST):
            raw[pl.ds(i * side, side)] = tile(i + 1, 0)

        @pl.when(p == 0)
        def _():
            top[...] = tile(0, 0)

    pl.semaphore_wait(barrier, rows + cols - 2)

    top_piece = side // pieces
    raw_piece = LOWER_MOST * side // pieces
    top_scatter, raw_scatter = fresh(pieces), fresh(pieces)
    top_spread = fresh(rows)
    top_gather, raw_gather = fresh(cols), fresh(cols)
    for j in range(pieces - 1, 0, -1):
        begin((q == 0) & (p == 0), lambda j=j: remote(
            span(top, j, top_piece), span(top, j, top_piece), top_scatter + j, {"pcol": j}))
    for j in range(pieces - 1, 0, -1):
        begin(q == 0, lambda j=j: remote(
            span(raw, j, raw_piece), span(raw, j, raw_piece), raw_scatter + j, {"pcol": j}))

    partner = {"prow": p + 1 - 2 * core}
    level0 = [fresh(2) for c in range(width)]

    def contribute(c):
        total = dot(pick[0], tile(0, c))
        for k in range(1, height):
            total = total + dot(pick[k], tile(k, c))
        part[c] = total.astype(jnp.bfloat16)

    for c in panel_cols:
        contribute(c)

        @pl.when(p == 0)
        def _():
            old[c] = tile(0, c)

        begin(None, lambda c=c: remote(part.at[c], recv.at[0, c], level0[c], partner))
        begin(p == 0, lambda c=c: remote(old.at[c], old.at[c], level0[c] + 1, {"prow": 1}))

    def low(level):
        return p < (1 << level)

    def high(level):
        return (p >= (1 << level)) & (p < (2 << level))

    sems = {}

    def level_send(level, c):
        peer = {"prow": p + (1 << level) - 2 * (1 << level) * lax.rem(p // (1 << level), 2)}
        last = level == levels - 1
        sems[level, c] = fresh(4)
        index = sems[level, c]
        before = part if level == 1 else send.at[level - 2]
        if level == 1:
            arrived(p == 1, lambda: remote(old.at[c], old.at[c], level0[c] + 1, {"prow": 0}))
            arrived(None, lambda: remote(part.at[c], recv.at[0, c], level0[c], partner))
        total = before[c].astype(jnp.float32) + recv[level - 1, c].astype(jnp.float32)
        send[level - 1, c] = total.astype(jnp.bfloat16)
        if last:
            @pl.when(p < rows // 2)
            def _():
                new[c] = jnp.where(owner_high, old[c].astype(jnp.float32), total).astype(jnp.bfloat16)

            @pl.when(p >= rows // 2)
            def _():
                new[c] = total.astype(jnp.bfloat16)

        src = new.at[c] if last else send.at[level - 1, c]
        begin(None, lambda: remote(span(src, core, half), span(recv.at[level, c], core, half), index, peer))
        if not last:
            begin(low(level),
                  lambda: remote(span(old.at[c], core, half), span(old.at[c], core, half), index + 1, peer))

    def level_forward(level, c):
        index = sems[level, c]
        here = span(recv.at[level, c], core, half)
        arrived(None, lambda: remote(here, here, index, partner))
        begin(None, lambda: remote(here, here, index + 2, partner))
        if level < levels - 1:
            mine = span(old.at[c], core, half)
            arrived(high(level), lambda: remote(mine, mine, index + 1, partner))
            begin(high(level), lambda: remote(mine, mine, index + 3, partner))

    def level_done(level, c):
        index = sems[level, c]
        there = span(recv.at[level, c], 1 - core, half)
        arrived(None, lambda: remote(there, there, index + 2, partner))
        if level < levels - 1:
            theirs = span(old.at[c], 1 - core, half)
            arrived(high(level), lambda: remote(theirs, theirs, index + 3, partner))

    for c in panel_cols:
        level_send(1, c)

    for j in range(1, pieces):
        arrived((q == j) & (p == 0), lambda j=j: remote(
            span(top, j, top_piece), span(top, j, top_piece), top_scatter + j, {"pcol": 0}))
    mine_top = span(top, q, top_piece)
    for d in range(1, rows):
        begin((p == 0) & (q < pieces), lambda d=d: remote(mine_top, mine_top, top_spread + d, {"prow": d}))

    def top_relay(cond):
        for d in range(1, cols):
            to = lax.rem(q + d, cols)
            begin(cond & (q < pieces) & ((to != 0) | (p != 0)),
                  lambda d=d, to=to: remote(mine_top, mine_top, top_gather + d, {"pcol": to}))

    for j in range(1, pieces):
        arrived(q == j, lambda j=j: remote(
            span(raw, j, raw_piece), span(raw, j, raw_piece), raw_scatter + j, {"pcol": 0}))
    mine_raw = span(raw, q, raw_piece)
    for d in range(1, cols):
        to = lax.rem(q + d, cols)
        begin((q < pieces) & (to != 0),
              lambda d=d, to=to: remote(mine_raw, mine_raw, raw_gather + d, {"pcol": to}))
    for d in range(1, rows):
        arrived((p == d) & (q < pieces), lambda d=d: remote(mine_top, mine_top, top_spread + d, {"prow": 0}))
    top_relay(p >= 0)

    l_sem, u_sem, corner_sem = fresh(cols), fresh(rows), fresh(rows)
    for d in range(1, cols):
        begin(None, lambda d=d: remote(lt.at[q], lt.at[q], l_sem + d, {"pcol": lax.rem(q + d, cols)}))
    mine_u = span(uf, p, u_rows)
    for d in range(1, rows):
        begin(None, lambda d=d: remote(mine_u, mine_u, u_sem + d, {"prow": lax.rem(p + d, rows)}))

    @pl.when(q == 0)
    def _():
        contribute(0)

    for d in range(1, rows):
        begin((q == 0) & (p == d), lambda d=d: remote(part.at[0], corner.at[d - 1], corner_sem + d, {"prow": 0}))

    for level in range(1, levels):
        if level > 1:
            for c in panel_cols:
                level_send(level, c)
        for c in panel_cols:
            level_forward(level, c)
        if level < levels - 1:
            for c in panel_cols:
                level_done(level, c)

    for d in range(1, cols):
        frm = lax.rem(q + cols - d, cols)
        remote(lt.at[frm], lt.at[frm], l_sem + d, {"pcol": frm}).wait_recv()
    lower_t = lt[...].astype(jnp.float32).reshape(side, side).astype(jnp.bfloat16)

    hit = [piv_lanes == sub + b for b in base]
    moved = [jnp.max(h.astype(jnp.float32), axis=1, keepdims=True) > 0.5 for h in hit]
    choose = [h.astype(jnp.float32).astype(jnp.bfloat16) for h in hit]

    def swap(k, block, source_rows):
        return jnp.where(moved[k], dot(choose[k], source_rows), block.astype(jnp.float32)).astype(jnp.bfloat16)

    for c in panel_cols:
        level_done(levels - 1, c)
        fresh_top = jnp.where(same, send[levels - 2, c].astype(jnp.float32),
                              recv[levels - 1, c].astype(jnp.float32)).astype(jnp.bfloat16)
        store[slots + c] = dot(lower_t, fresh_top, TN).astype(jnp.bfloat16)

        @pl.when(mine_high)
        def _():
            old[c] = recv[levels - 1, c]

        for k in range(1, height):
            store[slots + k * width + c] = swap(k, tile(k, c), old[c])

    for d in range(1, rows):
        frm = lax.rem(p + rows - d, rows)
        there = span(uf, frm, u_rows)
        remote(there, there, u_sem + d, {"prow": frm}).wait_recv()

    @pl.when((q == 0) & (p == 0))
    def _():
        total = part[0].astype(jnp.float32)
        for d in range(1, rows):
            remote(part.at[0], corner.at[d - 1], corner_sem + d, {"prow": d}).wait_recv()
            total = total + corner[d - 1].astype(jnp.float32)
        store[slots] = total.astype(jnp.bfloat16)

    for d in range(1, cols):
        frm = lax.rem(q + cols - d, cols)
        arrived((frm < pieces) & ((q != 0) | (p != 0)), lambda d=d, frm=frm: remote(
            span(top, frm, top_piece), span(top, frm, top_piece), top_gather + d, {"pcol": frm}))
    for d in range(1, cols):
        frm = lax.rem(q + cols - d, cols)
        arrived((q != 0) & (frm < pieces), lambda d=d, frm=frm: remote(
            span(raw, frm, raw_piece), span(raw, frm, raw_piece), raw_gather + d, {"pcol": frm}))
    for k in range(1, height):
        block = swap(k, raw[pl.ds((k - 1) * side, side)], top[...])
        lower = dot(block, uf[...]).astype(jnp.bfloat16)
        store[slots + k * width] = lower
        for c in panel_cols:
            at = slots + k * width + c
            store[at] = (store[at].astype(jnp.float32) - dot(lower, store[slots + c])).astype(jnp.bfloat16)

    for s in range(slots):
        out_ref[0, 0, s] = store[source[s]]
    for cond, make in ends:
        guard(cond, lambda make=make: make().wait_send())


def body(tiles, tile_ids, counts, pivots, l_inverse, u_inverse):
    rows = lax.axis_size("prow")
    cols = lax.axis_size("pcol")
    side = pivots.shape[0]
    slots = tiles.shape[2]
    grid_cols = LOCAL_ROWS * rows // cols
    levels = rows.bit_length() - 1
    width = UPPER_MOST + 1
    height = LOWER_MOST + 1
    block = (side, side)
    pieces = min(cols, 16)
    count = 3 * rows + 2 * pieces + 3 * cols + width * (2 + 4 * (levels - 1))
    kind = jnp.bfloat16
    hbm = pl.BlockSpec(memory_space=pltpu.HBM)
    return pl.pallas_call(
        functools.partial(kernel, rows, cols, grid_cols),
        out_shape=jax.ShapeDtypeStruct(tiles.shape, tiles.dtype),
        in_specs=[hbm] * 6,
        out_specs=pl.BlockSpec(memory_space=pltpu.VMEM),
        scratch_shapes=[
            pltpu.SMEM(tile_ids.shape, jnp.int32),
            pltpu.SMEM(counts.shape, jnp.int32),
            pltpu.VMEM((1, side), jnp.int32),
            pltpu.VMEM((slots + height * width + 1,) + block, kind),
            pltpu.VMEM((width,) + block, kind),
            pltpu.VMEM((width,) + block, kind),
            pltpu.VMEM((levels - 1, width) + block, kind),
            pltpu.VMEM((levels, width) + block, kind),
            pltpu.VMEM((width,) + block, kind),
            pltpu.VMEM((LOWER_MOST * side, side), kind),
            pltpu.VMEM(block, kind),
            pltpu.VMEM((cols, side // cols, side), kind),
            pltpu.VMEM(block, kind),
            pltpu.VMEM((rows - 1,) + block, kind),
            pltpu.SemaphoreType.DMA((6,)),
            pltpu.SemaphoreType.DMA((count,)),
            pltpu.SemaphoreType.DMA((count,)),
        ],
        compiler_params=pltpu.CompilerParams(
            collective_id=0, has_side_effects=True, vmem_limit_bytes=48 * 1024 * 1024
        ),
    )(tile_ids, counts, pivots.reshape(1, side), l_inverse.T, u_inverse, tiles)


def solution(mesh):
    placed = (
        P("prow", "pcol", None, None, None),
        P("prow", "pcol", None),
        P("prow", "pcol"),
        P(),
        P(None, "pcol"),
        P("prow", None),
    )
    return jax.shard_map(
        body,
        mesh=mesh,
        in_specs=placed,
        out_specs=P("prow", "pcol", None, None, None),
        check_vma=False,
    )
```

time: 36.7 us -> 37.8 us (1.030)
  Pallas kernels: 29.6 us -> 31.2 us
    pallas_call x1, Pallas kernels: 29.6 us -> 31.2 us  [body(): pl.pallas_call(functools.partial(kernel, rows, cols, grid_cols), out_shap...]
    unnamed x10 -> x11, local copies, waits for them, and re-layouts: 5.84 us -> 5.71 us
where the time goes in v1:
time: 37.8 us; the launch traced here: 37.5 us
  Pallas kernels  31.2 us (83%)
  local copies, waits for them, and re-layouts  5.71 us (15%)
  between operations  0.67 us (2%)
    pallas_call x1, Pallas kernels, body(): pl.pallas_call(functools.partial(kernel, rows, cols, grid_cols), out_shap...  31.2 us
    unnamed x11, local copies, waits for them, and re-layouts  5.71 us

profile of v1, /device:TPU:26, one launch (start us, length us, event | category | flops | bytes accessed | tf_op | source)
XLA Modules:
  0.0 37.5 jit_solution(16901887238575232991)
XLA Ops:
  0.7 0.0 copy-start
  0.7 1.6 %copy-done = bf16[1,1,16,256,256]{4,3,2,1,0:T(8,128)(2,1)S(1)} copy-done((bf16[1,1,16,256,256]{4,3,2,1,0:T(8,128)(2,1)S(1)}, bf16[1,1,16,256,256]{4,3,2,1,0:T(8,128)(2,1)}, u32[]{:S(2)}) %copy-start) | copy-done | bytes 2097176
  2.2 0.0 copy-start.1
  2.2 0.8 %copy-done.1 = bf16[64,256]{1,0:T(8,128)(2,1)S(1)} copy-done((bf16[64,256]{1,0:T(8,128)(2,1)S(1)}, bf16[64,256]{1,0:T(8,128)(2,1)}, u32[]{:S(2)}) %copy-start.1) | copy-done | bytes 32792
  3.0 0.0 copy-start.2
  3.0 0.7 %copy-done.2 = bf16[256,32]{0,1:T(8,128)(2,1)S(1)} copy-done((bf16[256,32]{0,1:T(8,128)(2,1)S(1)}, bf16[256,32]{0,1:T(8,128)(2,1)}, u32[]{:S(2)}) %copy-start.2) | copy-done | bytes 16408
  3.7 0.0 copy-start.3
  3.7 0.7 %copy-done.3 = s32[256]{0:T(256)S(1)} copy-done((s32[256]{0:T(256)S(1)}, s32[256]{0:T(256)}, u32[]{:S(2)}) %copy-start.3) | copy-done | bytes 1048
  4.4 0.0 copy-start.4
  4.4 0.7 %copy-done.4 = s32[1,1,16]{2,1,0:T(1,128)S(1)} copy-done((s32[1,1,16]{2,1,0:T(1,128)S(1)}, s32[1,1,16]{2,1,0:T(1,128)}, u32[]{:S(2)}) %copy-start.4) | copy-done | bytes 88
  5.1 31.2 %shard_map.64 = bf16[1,1,16,256,256]{4,3,2,1,0:T(8,128)(2,1)S(1)} custom-call(s32[1,1,16]{2,1,0:T(1,128)S(1)} %copy-done.4, s32[1,1]{1,0:T(1,128)S(6)} %copy.8.counts_hbm, s32[1,256]{1,0:T(1,128)S(1)} %bitcast.3, bf16[32,256]{1,0:T(8,128)(2,1)S(1)} %bitcast.2, bf16[64,256]{1,0:T(8,128)(2,1)S(1)} %copy-done.1, bf16[1,1,16,256,256]{4,3,2,1,0:T(8,128)(2,1)S(1)} %copy-done), custom_call_target="tpu_custom_call" | custom-call | tf_op jit(solution)/shard_map/pallas_call | solution.py:356
  36.2 1.3 %copy.9 = bf16[1,1,16,256,256]{4,3,2,1,0:T(8,128)(2,1)} copy(bf16[1,1,16,256,256]{4,3,2,1,0:T(8,128)(2,1)S(1)} %shard_map.64) | data formatting | bytes 4194304
Async XLA Ops:
  0.7 1.6 %copy-start = (bf16[1,1,16,256,256]{4,3,2,1,0:T(8,128)(2,1)S(1)}, bf16[1,1,16,256,256]{4,3,2,1,0:T(8,128)(2,1)}, u32[]{:S(2)}) copy-start(bf16[1,1,16,256,256]{4,3,2,1,0:T(8,128)(2,1)} %tiles_hbm.1) | copy-start | bytes 6291460
  2.2 0.8 %copy-start.1 = (bf16[64,256]{1,0:T(8,128)(2,1)S(1)}, bf16[64,256]{1,0:T(8,128)(2,1)}, u32[]{:S(2)}) copy-start(bf16[64,256]{1,0:T(8,128)(2,1)} %u_hbm.1) | copy-start | bytes 98308
  3.0 0.7 %copy-start.2 = (bf16[256,32]{0,1:T(8,128)(2,1)S(1)}, bf16[256,32]{0,1:T(8,128)(2,1)}, u32[]{:S(2)}) copy-start(bf16[256,32]{0,1:T(8,128)(2,1)} %param.10) | copy-start | bytes 49156
  3.7 0.7 %copy-start.3 = (s32[256]{0:T(256)S(1)}, s32[256]{0:T(256)}, u32[]{:S(2)}) copy-start(s32[256]{0:T(256)} %param.9) | copy-start | bytes 3076
  4.4 0.7 %copy-start.4 = (s32[1,1,16]{2,1,0:T(1,128)S(1)}, s32[1,1,16]{2,1,0:T(1,128)}, u32[]{:S(2)}) copy-start(s32[1,1,16]{2,1,0:T(1,128)} %ids_hbm.1) | copy-start | bytes 196

commit v2 on v1

--- a/solution.py
+++ b/solution.py
@@ -24,9 +24,9 @@
 
 def kernel(
     rows, cols, grid_cols,
-    ids_hbm, counts_hbm, piv_hbm, l_hbm, u_hbm, tiles_hbm,
+    counts_ref, ids_hbm, piv_hbm, l_hbm, u_hbm, tiles_hbm,
     out_ref,
-    ids_ref, counts_ref, piv_ref,
+    ids_ref, piv_ref,
     store, part, old, send, recv, new, raw, top, lt, uf, corner,
     in_sem, ss, rs,
 ):
@@ -75,15 +75,14 @@
     tile_copy = pltpu.make_async_copy(tiles_hbm.at[0, 0], store.at[pl.ds(0, slots)], in_sem.at[0])
     inputs = [
         pltpu.make_async_copy(ids_hbm, ids_ref, in_sem.at[1]),
-        pltpu.make_async_copy(counts_hbm, counts_ref, in_sem.at[2]),
         pltpu.make_async_copy(piv_hbm, piv_ref, in_sem.at[3]),
         pltpu.make_async_copy(l_hbm, lt.at[q], in_sem.at[4]),
         pltpu.make_async_copy(u_hbm, span(uf, p, u_rows), in_sem.at[5]),
     ]
-    for copy in inputs[:3]:
+    for copy in inputs[:2]:
         copy.start()
     tile_copy.start()
-    for copy in inputs[3:]:
+    for copy in inputs[2:]:
         copy.start()
 
     barrier = pltpu.get_barrier_semaphore()
@@ -352,15 +351,15 @@
     pieces = min(cols, 16)
     count = 3 * rows + 2 * pieces + 3 * cols + width * (2 + 4 * (levels - 1))
     kind = jnp.bfloat16
+    operands = (tile_ids, pivots.reshape(1, side), l_inverse.T, u_inverse, tiles)
     hbm = pl.BlockSpec(memory_space=pltpu.HBM)
     return pl.pallas_call(
         functools.partial(kernel, rows, cols, grid_cols),
         out_shape=jax.ShapeDtypeStruct(tiles.shape, tiles.dtype),
-        in_specs=[hbm] * 6,
+        in_specs=[pl.BlockSpec(memory_space=pltpu.SMEM)] + [hbm] * 5,
         out_specs=pl.BlockSpec(memory_space=pltpu.VMEM),
         scratch_shapes=[
             pltpu.SMEM(tile_ids.shape, jnp.int32),
-            pltpu.SMEM(counts.shape, jnp.int32),
             pltpu.VMEM((1, side), jnp.int32),
             pltpu.VMEM((slots + height * width + 1,) + block, kind),
             pltpu.VMEM((width,) + block, kind),
@@ -380,7 +379,7 @@
         compiler_params=pltpu.CompilerParams(
             collective_id=0, has_side_effects=True, vmem_limit_bytes=48 * 1024 * 1024
         ),
-    )(tile_ids, counts, pivots.reshape(1, side), l_inverse.T, u_inverse, tiles)
+    )(counts, *[pltpu.with_memory_space_constraint(a, pltpu.HBM) for a in operands])
 
 
 def solution(mesh):

time: 37.8 us -> 33.1 us (0.88)
  local copies, waits for them, and re-layouts: 5.71 us -> 1.32 us
    unnamed x11 -> x1, local copies, waits for them, and re-layouts: 5.71 us -> 1.32 us
where the time goes in v2:
time: 33.1 us; the launch traced here: 33 us
  Pallas kernels  31 us (94%)
  local copies, waits for them, and re-layouts  1.32 us (4%)
  between operations  0.66 us (2%)
    pallas_call x1, Pallas kernels, body(): pl.pallas_call(functools.partial(kernel, rows, cols, grid_cols), out_shap...  31 us
    unnamed x1, local copies, waits for them, and re-layouts  1.32 us

profile of v2, /device:TPU:26, one launch (start us, length us, event | category | flops | bytes accessed | tf_op | source)
XLA Modules:
  0.0 33.0 jit_solution(17100548184592929411)
XLA Ops:
  0.7 31.0 %shard_map.64 = bf16[1,1,16,256,256]{4,3,2,1,0:T(8,128)(2,1)S(1)} custom-call(s32[1,1]{1,0:T(1,128)S(6)} %copy.8.counts_ref, s32[1,1,16]{2,1,0:T(1,128)} %ids_hbm.1, s32[1,256]{1,0:T(1,128)} %bitcast.3, bf16[32,256]{1,0:T(8,128)(2,1)} %bitcast.2, bf16[64,256]{1,0:T(8,128)(2,1)} %u_hbm.1, bf16[1,1,16,256,256]{4,3,2,1,0:T(8,128)(2,1)} %tiles_hbm.1), custom_call_target="tpu_custom_call" | custom-call | tf_op jit(solution)/shard_map/pallas_call | solution.py:356
  31.6 1.3 %copy.9 = bf16[1,1,16,256,256]{4,3,2,1,0:T(8,128)(2,1)} copy(bf16[1,1,16,256,256]{4,3,2,1,0:T(8,128)(2,1)S(1)} %shard_map.64) | data formatting | bytes 4194304

commit v3 on v2

--- a/solution.py
+++ b/solution.py
@@ -246,7 +246,10 @@
         arrived(q == j, lambda j=j: remote(
             span(raw, j, raw_piece), span(raw, j, raw_piece), raw_scatter + j, {"pcol": 0}))
     mine_raw = span(raw, q, raw_piece)
-    for d in range(1, cols):
+    twin = q + 1 - 2 * lax.rem(q, 2)
+    raw_twin = fresh(cols)
+    begin((q < pieces) & (twin != 0), lambda: remote(mine_raw, mine_raw, raw_twin, {"pcol": twin}))
+    for d in range(2, cols, 2):
         to = lax.rem(q + d, cols)
         begin((q < pieces) & (to != 0),
               lambda d=d, to=to: remote(mine_raw, mine_raw, raw_gather + d, {"pcol": to}))
@@ -278,6 +281,14 @@
             for c in panel_cols:
                 level_done(level, c)
 
+    for d in range(2, cols, 2):
+        frm = lax.rem(q + cols - d, cols)
+        there = span(raw, frm, raw_piece)
+        arrived((q != 0) & (frm < pieces), lambda d=d, there=there, frm=frm: remote(
+            there, there, raw_gather + d, {"pcol": frm}))
+        begin((twin != 0) & (frm < pieces), lambda d=d, there=there: remote(
+            there, there, raw_twin + d, {"pcol": twin}))
+
     for d in range(1, cols):
         frm = lax.rem(q + cols - d, cols)
         remote(lt.at[frm], lt.at[frm], l_sem + d, {"pcol": frm}).wait_recv()
@@ -320,10 +331,11 @@
         frm = lax.rem(q + cols - d, cols)
         arrived((frm < pieces) & ((q != 0) | (p != 0)), lambda d=d, frm=frm: remote(
             span(top, frm, top_piece), span(top, frm, top_piece), top_gather + d, {"pcol": frm}))
-    for d in range(1, cols):
-        frm = lax.rem(q + cols - d, cols)
-        arrived((q != 0) & (frm < pieces), lambda d=d, frm=frm: remote(
-            span(raw, frm, raw_piece), span(raw, frm, raw_piece), raw_gather + d, {"pcol": frm}))
+    for d in range(0, cols, 2):
+        frm = lax.rem(twin + cols - d, cols)
+        there = span(raw, frm, raw_piece)
+        arrived((q != 0) & (frm < pieces), lambda d=d, there=there: remote(
+            there, there, raw_twin + d, {"pcol": twin}))
     for k in range(1, height):
         block = swap(k, raw[pl.ds((k - 1) * side, side)], top[...])
         lower = dot(block, uf[...]).astype(jnp.bfloat16)
@@ -349,7 +361,7 @@
     height = LOWER_MOST + 1
     block = (side, side)
     pieces = min(cols, 16)
-    count = 3 * rows + 2 * pieces + 3 * cols + width * (2 + 4 * (levels - 1))
+    count = 3 * rows + 2 * pieces + 4 * cols + width * (2 + 4 * (levels - 1))
     kind = jnp.bfloat16
     operands = (tile_ids, pivots.reshape(1, side), l_inverse.T, u_inverse, tiles)
     hbm = pl.BlockSpec(memory_space=pltpu.HBM)

time: 33.1 us -> 28.8 us (0.87)
  Pallas kernels: 31 us -> 26.7 us
    pallas_call x1, Pallas kernels: 31 us -> 26.7 us  [body(): pl.pallas_call(functools.partial(kernel, rows, cols, grid_cols), out_shap...]
where the time goes in v3:
time: 28.8 us; the launch traced here: 28.6 us
  Pallas kernels  26.7 us (93%)
  local copies, waits for them, and re-layouts  1.32 us (5%)
  between operations  0.66 us (2%)
    pallas_call x1, Pallas kernels, body(): pl.pallas_call(functools.partial(kernel, rows, cols, grid_cols), out_shap...  26.7 us
    unnamed x1, local copies, waits for them, and re-layouts  1.32 us

profile of v3, /device:TPU:26, one launch (start us, length us, event | category | flops | bytes accessed | tf_op | source)
XLA Modules:
  0.0 28.6 jit_solution(5316700545035995130)
XLA Ops:
  0.7 26.7 %shard_map.64 = bf16[1,1,16,256,256]{4,3,2,1,0:T(8,128)(2,1)S(1)} custom-call(s32[1,1]{1,0:T(1,128)S(6)} %copy.8.counts_ref, s32[1,1,16]{2,1,0:T(1,128)} %ids_hbm.1, s32[1,256]{1,0:T(1,128)} %bitcast.3, bf16[32,256]{1,0:T(8,128)(2,1)} %bitcast.2, bf16[64,256]{1,0:T(8,128)(2,1)} %u_hbm.1, bf16[1,1,16,256,256]{4,3,2,1,0:T(8,128)(2,1)} %tiles_hbm.1), custom_call_target="tpu_custom_call" | custom-call | tf_op jit(solution)/shard_map/pallas_call | solution.py:368
  27.3 1.3 %copy.9 = bf16[1,1,16,256,256]{4,3,2,1,0:T(8,128)(2,1)} copy(bf16[1,1,16,256,256]{4,3,2,1,0:T(8,128)(2,1)S(1)} %shard_map.64) | data formatting | bytes 4194304
